TPU v7x, 32 devices: a whole 2x2x4 slice. The times are simulated.
32 devices in a mesh: gx: 4 (over x, core), gy: 4 (over z), gz: 2 (over y).
Axes of the slice: x: 2, y: 2, z: 4, core: 2. Of those that a mesh axis runs over, the one named last changes fastest.
Arguments:
- fields: float32 [11, 500, 32, 256], P(None, 'gx', 'gy', 'gz'), may hold values from -6 to 6
- var_scale: float32 [11], replicated, may hold values from 0.3 to 3
- start_basis: float32 [500, 64], replicated, may hold values from -6 to 6
Outputs:
- factor: float32 [500, 64], replicated
- core: float32 [64, 11, 32, 256], P('gx', None, 'gy', 'gz')
All inputs are finite; a program needn't handle non-finite values.
Results may differ from a plain program's by a relative error of at most 0.0002.
Values sent between devices are 32-bit elements; how exact they have to be, the bound alone decides.
A program may use at most 128 MiB of HBM per device.

v0:
```python
import jax
import jax.numpy as jnp
from jax import lax
from jax.sharding import PartitionSpec as P

ITERS = 3


def orthonormal(block):
    small = jnp.dot(block.T, block, precision=lax.Precision.HIGHEST)
    lower = jnp.linalg.cholesky(small)
    return jax.scipy.linalg.solve_triangular(lower, block.T, lower=True).T


def per_device(fields, var_scale, start_basis):
    scaled = fields * var_scale[:, None, None, None]
    rows_dev = scaled.shape[1]
    contract = (((0, 2, 3), (0, 2, 3)), ((), ()))
    swapped = lax.all_to_all(scaled, "gx", split_axis=2, concat_axis=1, tiled=True)
    partial_gram = lax.dot_general(swapped, swapped, contract, precision=lax.Precision.HIGHEST)
    gram = lax.psum(partial_gram, ("gx", "gy", "gz"))
    basis = start_basis
    for step in range(ITERS):
        basis = orthonormal(jnp.dot(gram, basis, precision=lax.Precision.HIGHEST))
    along_rows = (((0,), (1,)), ((), ()))
    own_basis = lax.dynamic_slice_in_dim(basis, lax.axis_index("gx") * rows_dev, rows_dev, 0)
    core = lax.psum_scatter(
        lax.dot_general(own_basis, scaled, along_rows, precision=lax.Precision.HIGHEST),
        "gx",
        scatter_dimension=0,
        tiled=True,
    )
    return (basis, core)


def solution(mesh):
    in_specs = (P(None, "gx", "gy", "gz"), P(), P())
    out_specs = (P(), P("gx", None, "gy", "gz"))
    return jax.shard_map(
        per_device, mesh=mesh, in_specs=in_specs, out_specs=out_specs, check_vma=False
    )
```

profile of v0, /device:TPU:0, one launch (start us, length us, event | category | flops | bytes accessed | tf_op | source)
XLA Modules:
  0.0 333.2 jit_solution(15597270235788873526)
XLA Ops:
  7.2 3.1 broadcast_multiply_fusion
  10.3 1.1 copy.24
  11.4 1.3 copy-done.1
  12.7 69.0 %all_to_all.18 = f32[11,125,8,128]{3,1,0,2:T(8,128)S(1)} all-to-all(f32[11,125,8,128]{3,1,0,2:T(8,128)S(1)} %copy.24), channel_id=1, replica_groups=mesh['gx'=4,'gy'=4,'gz'=2] {'gx'}, dimensions={2} | all-to-all | bytes 11264000 | tf_op jit(solution)/shard_map/all_to_all | solution.py:19
  81.7 2.9 copy.36
  84.6 6.2 %all_to_all.16 = f32[11,500,2,128]{3,1,2,0:T(8,128)} reshape(f32[11,4,125,2,128]{4,2,1,3,0:T(8,128)} %bitcast.67) | data formatting | bytes 11264000 | tf_op jit(solution)/shard_map/all_to_all | solution.py:19
  90.8 13.6 %convolution_bitcast_fusion = f32[500,500]{1,0:T(8,128)} fusion(f32[11,500,2,128]{3,1,2,0:T(8,128)} %all_to_all.16), kind=kOutput, calls=%fused_computation.4 | convolution fusion | flops 8448000000 | bytes 6632000 | tf_op jit(solution)/shard_map/dot_general | solution.py:20
  104.7 130.7 %all-reduce.2.cloned.1.call-done = f32[500,500]{1,0:T(8,128)} async-done(((f32[500,500]{1,0:T(8,128)}), f32[500,500]{1,0:T(8,128)}) %all-reduce.2.cloned.1.call-update) | async-done | bytes 1000016 | tf_op jit(solution)/shard_map/psum | solution.py:21
  235.4 2.3 fusion.24
  238.0 5.8 %cholesky.59 = f32[64,64]{1,0:T(8,128)S(1)} custom-call(f32[64,64]{1,0:T(8,128)S(1)} %fusion.17), custom_call_target="Cholesky" | custom-call | tf_op jit(solution)/shard_map/jit(cholesky)/cholesky | solution.py:11
  243.9 0.6 compare_reduce_fusion.2
  244.6 0.7 fusion.8
  245.2 4.9 %custom-call.7 = f32[1,64,64]{1,2,0:T(8,128)S(1)} custom-call(f32[1,64,64]{2,1,0:T(8,128)S(1)} %fusion.8), custom_call_target="InvertDiagBlocksLowerTriangular" | custom-call | tf_op jit(solution)/shard_map/jit(_solve_triangular)/triangular_solve | solution.py:12
  250.5 2.3 fusion.26
  253.1 5.8 %cholesky.70 = f32[64,64]{1,0:T(8,128)S(1)} custom-call(f32[64,64]{1,0:T(8,128)S(1)} %fusion.15), custom_call_target="Cholesky" | custom-call | tf_op jit(solution)/shard_map/jit(cholesky)/cholesky | solution.py:11
  259.6 0.7 fusion.9
  260.3 4.9 %custom-call.8 = f32[1,64,64]{1,2,0:T(8,128)S(1)} custom-call(f32[1,64,64]{2,1,0:T(8,128)S(1)} %fusion.9), custom_call_target="InvertDiagBlocksLowerTriangular" | custom-call | tf_op jit(solution)/shard_map/jit(_solve_triangular)/triangular_solve | solution.py:12
  265.5 2.3 fusion.28
  268.2 5.8 %cholesky.81 = f32[64,64]{1,0:T(8,128)S(1)} custom-call(f32[64,64]{1,0:T(8,128)S(1)} %fusion.13), custom_call_target="Cholesky" | custom-call | tf_op jit(solution)/shard_map/jit(cholesky)/cholesky | solution.py:11
  274.7 0.7 fusion.10
  275.4 4.9 %custom-call.9 = f32[1,64,64]{1,2,0:T(8,128)S(1)} custom-call(f32[1,64,64]{2,1,0:T(8,128)S(1)} %fusion.10), custom_call_target="InvertDiagBlocksLowerTriangular" | custom-call | tf_op jit(solution)/shard_map/jit(_solve_triangular)/triangular_solve | solution.py:12
  280.6 8.3 %fusion = f32[64,11,8,128]{3,0,2,1:T(8,128)} fusion(f32[11,125,8,128]{3,2,1,0:T(8,128)} %copy-done.1, f32[64,500]{1,0:T(8,128)S(1)} %fusion.2, s32[]{:T(128)S(6)} %select_n.6), kind=kOutput, calls=%fused_computation | convolution fusion | flops 1081344000 | bytes 8548356 | tf_op jit(solution)/shard_map/dot_general | solution.py:28
  288.9 35.2 %reduce-scatter.2.cloned.1.call-done = f32[16,11,8,128]{3,0,2,1:T(8,128)} async-done(((f32[64,11,8,128]{3,0,2,1:T(8,128)}), f32[16,11,8,128]{3,0,2,1:T(8,128)}) %reduce-scatter.2.cloned.1.call-update) | async-done | bytes 720912 | tf_op jit(solution)/shard_map/reduce_scatter | solution.py:27
  324.2 2.2 copy.30
  (26 shorter events, 3.7 us)
Async XLA Ops:
  7.2 228.2 %copy-start = (f32[500,64]{0,1:T(8,128)S(1)}, f32[500,64]{0,1:T(8,128)}, u32[]{:S(2)}) copy-start(f32[500,64]{0,1:T(8,128)} %param.8) | copy-start | bytes 384004
  7.2 228.2 %all-reduce.2.cloned.1.call-start = ((), (), s32[]{:S(2)}) async-start(), calls=%async_computation.2 | async-start | bytes 2064384 | tf_op jit(solution)/shard_map/psum | solution.py:21
  10.3 2.4 copy-start.1
  104.4 219.7 %reduce-scatter.2.cloned.1.call-start = ((), (), s32[]{:S(2)}) async-start(), calls=%async_computation.3 | async-start | bytes 3604480 | tf_op jit(solution)/shard_map/reduce_scatter | solution.py:27
  280.6 8.3 %copy-start.2 = (f32[64,500]{1,0:T(8,128)}, f32[64,500]{1,0:T(8,128)S(1)}, u32[]{:S(2)}) copy-start(f32[64,500]{1,0:T(8,128)S(1)} %fusion.2) | copy-start | bytes 384004
Sparse Core Ops, SparseCore 0:
  104.6 130.7 all-reduce.1
  289.0 35.0 reduce-scatter.1
where the time goes:
time: 334 us; the launch traced here: 333 us
  waiting for transfers between devices  166 us (50%)
  blocking collectives  69 us (21%)
  other arithmetic  39.3 us (12%)
  matrix products  30.5 us (9%)
  between operations  14.2 us (4%)
  local copies, waits for them, and re-layouts  13.9 us (4%)
    psum x1, waiting for transfers between devices, per_device(): gram = lax.psum(partial_gram, ('gx', 'gy', 'gz'))  131 us
    all_to_all x1, blocking collectives, per_device(): lax.all_to_all(scaled, 'gx', split_axis=2, concat_axis=1, tiled=True)  69 us
    reduce_scatter x1, waiting for transfers between devices, per_device(): lax.psum_scatter(lax.dot_general(own_basis, scaled, along_rows, precision...  35.2 us
    another operation x9, other arithmetic, orthonormal(): lower = jnp.linalg.cholesky(small)  19.6 us
    another operation x6, other arithmetic, orthonormal(): return jax.scipy.linalg.solve_triangular(lower, block.T, lower=True).T  16.6 us
    dot_general x1, matrix products, per_device(): lax.dot_general(swapped, swapped, contract, precision=lax.Precision.HIGHEST)  13.6 us
    all_to_all x2, local copies, waits for them, and re-layouts, per_device(): lax.all_to_all(scaled, 'gx', split_axis=2, concat_axis=1, tiled=True)  9.05 us
    dot_general x1, matrix products, per_device(): lax.dot_general(own_basis, scaled, along_rows, precision=lax.Precision.HI...  8.26 us
  transfers between devices with their start and end apart: 2, of which 2 were waited for; matrix products, arithmetic and copies ran while one was open for 0% of the time, Pallas kernels for 0%

commit v1 on v0

--- a/solution.py
+++ b/solution.py
@@ -18,7 +18,8 @@
     contract = (((0, 2, 3), (0, 2, 3)), ((), ()))
     swapped = lax.all_to_all(scaled, "gx", split_axis=2, concat_axis=1, tiled=True)
     partial_gram = lax.dot_general(swapped, swapped, contract, precision=lax.Precision.HIGHEST)
-    gram = lax.psum(partial_gram, ("gx", "gy", "gz"))
+    parts = lax.all_gather(partial_gram, ("gx", "gy", "gz"), axis=0, tiled=False)
+    gram = parts.sum(axis=0)
     basis = start_basis
     for step in range(ITERS):
         basis = orthonormal(jnp.dot(gram, basis, precision=lax.Precision.HIGHEST))

time: 334 us -> 403 us (1.21)
  waiting for transfers between devices: 166 us -> 227 us
  other arithmetic: 39.3 us -> 51.4 us
    all_gather x0 -> x1, waiting for transfers between devices: none -> 192 us  [per_device(): lax.all_gather(partial_gram, ('gx', 'gy', 'gz'), axis=0, tiled=False)]
    psum x1 -> x0, waiting for transfers between devices: 131 us -> none  [per_device(): gram = lax.psum(partial_gram, ('gx', 'gy', 'gz'))]
    reduce_sum x0 -> x1, other arithmetic: none -> 12.2 us  [per_device(): gram = parts.sum(axis=0)]
where the time goes in v1:
time: 403 us; the launch traced here: 402 us
  waiting for transfers between devices  227 us (56%)
  blocking collectives  69 us (17%)
  other arithmetic  51.4 us (13%)
  matrix products  26.8 us (7%)
  between operations  14.2 us (4%)
  local copies, waits for them, and re-layouts  14 us (3%)
    all_gather x1, waiting for transfers between devices, per_device(): lax.all_gather(partial_gram, ('gx', 'gy', 'gz'), axis=0, tiled=False)  192 us
    all_to_all x1, blocking collectives, per_device(): lax.all_to_all(scaled, 'gx', split_axis=2, concat_axis=1, tiled=True)  69 us
    reduce_scatter x1, waiting for transfers between devices, per_device(): lax.psum_scatter(lax.dot_general(own_basis, scaled, along_rows, precision...  34.4 us
    another operation x9, other arithmetic, orthonormal(): lower = jnp.linalg.cholesky(small)  19.6 us
    another operation x6, other arithmetic, orthonormal(): return jax.scipy.linalg.solve_triangular(lower, block.T, lower=True).T  16.6 us
    dot_general x1, matrix products, per_device(): lax.dot_general(swapped, swapped, contract, precision=lax.Precision.HIGHEST)  13.6 us
    reduce_sum x1, other arithmetic, per_device(): gram = parts.sum(axis=0)  12.2 us
    all_to_all x2, local copies, waits for them, and re-layouts, per_device(): lax.all_to_all(scaled, 'gx', split_axis=2, concat_axis=1, tiled=True)  9.05 us
  transfers between devices with their start and end apart: 2, of which 2 were waited for; matrix products, arithmetic and copies ran while one was open for 0% of the time, Pallas kernels for 0%

profile of v1, /device:TPU:0, one launch (start us, length us, event | category | flops | bytes accessed | tf_op | source)
XLA Modules:
  0.0 402.2 jit_solution(17418091931119433425)
XLA Ops:
  7.2 3.1 broadcast_multiply_fusion
  10.3 1.1 copy.24
  11.4 1.4 copy-done.1
  12.8 69.0 %all_to_all.18 = f32[11,125,8,128]{3,1,0,2:T(8,128)S(1)} all-to-all(f32[11,125,8,128]{3,1,0,2:T(8,128)S(1)} %copy.24), channel_id=1, replica_groups=mesh['gx'=4,'gy'=4,'gz'=2] {'gx'}, dimensions={2} | all-to-all | bytes 11264000 | tf_op jit(solution)/shard_map/all_to_all | solution.py:19
  81.8 2.9 copy.36
  84.7 6.2 %all_to_all.16 = f32[11,500,2,128]{3,1,2,0:T(8,128)} reshape(f32[11,4,125,2,128]{4,2,1,3,0:T(8,128)} %bitcast.69) | data formatting | bytes 11264000 | tf_op jit(solution)/shard_map/all_to_all | solution.py:19
  90.9 13.6 %convolution_bitcast_fusion = f32[1,500,500]{2,1,0:T(8,128)} fusion(f32[11,500,2,128]{3,1,2,0:T(8,128)} %all_to_all.16), kind=kOutput, calls=%fused_computation.4 | convolution fusion | flops 8448000000 | bytes 6632000 | tf_op jit(solution)/shard_map/dot_general | solution.py:20
  104.6 192.2 %all-gather.4.cloned.1.call-done = f32[32,500,500]{2,1,0:T(8,128)} async-done(((f32[1,500,500]{2,1,0:T(8,128)}), f32[32,500,500]{2,1,0:T(8,128)}) %all-gather.4.cloned.1.call-update) | async-done | bytes 32000016 | tf_op jit(solution)/shard_map/all_gather | solution.py:21
  296.7 12.2 %reduce_sum.9 = f32[500,500]{1,0:T(8,128)S(1)} reduce(f32[32,500,500]{2,1,0:T(8,128)} %all-gather.4.cloned.1.call-done, f32[]{:T(128)} %constant.39.clone.1), dimensions={0}, to_apply=%region_0.0 | reduce | flops 7750000 | bytes 33000004 | tf_op jit(solution)/shard_map/reduce_sum | solution.py:22
  308.9 1.1 fusion.24
  310.3 5.8 %cholesky.59 = f32[64,64]{1,0:T(8,128)S(1)} custom-call(f32[64,64]{1,0:T(8,128)S(1)} %fusion.17), custom_call_target="Cholesky" | custom-call | tf_op jit(solution)/shard_map/jit(cholesky)/cholesky | solution.py:11
  316.9 0.7 fusion.8
  317.5 4.9 %custom-call.7 = f32[1,64,64]{1,2,0:T(8,128)S(1)} custom-call(f32[1,64,64]{2,1,0:T(8,128)S(1)} %fusion.8), custom_call_target="InvertDiagBlocksLowerTriangular" | custom-call | tf_op jit(solution)/shard_map/jit(_solve_triangular)/triangular_solve | solution.py:12
  322.8 1.1 fusion.26
  324.2 5.8 %cholesky.70 = f32[64,64]{1,0:T(8,128)S(1)} custom-call(f32[64,64]{1,0:T(8,128)S(1)} %fusion.15), custom_call_target="Cholesky" | custom-call | tf_op jit(solution)/shard_map/jit(cholesky)/cholesky | solution.py:11
  330.7 0.7 fusion.9
  331.4 4.9 %custom-call.8 = f32[1,64,64]{1,2,0:T(8,128)S(1)} custom-call(f32[1,64,64]{2,1,0:T(8,128)S(1)} %fusion.9), custom_call_target="InvertDiagBlocksLowerTriangular" | custom-call | tf_op jit(solution)/shard_map/jit(_solve_triangular)/triangular_solve | solution.py:12
  336.6 1.1 fusion.28
  338.0 5.8 %cholesky.81 = f32[64,64]{1,0:T(8,128)S(1)} custom-call(f32[64,64]{1,0:T(8,128)S(1)} %fusion.13), custom_call_target="Cholesky" | custom-call | tf_op jit(solution)/shard_map/jit(cholesky)/cholesky | solution.py:11
  344.6 0.7 fusion.10
  345.2 4.9 %custom-call.9 = f32[1,64,64]{1,2,0:T(8,128)S(1)} custom-call(f32[1,64,64]{2,1,0:T(8,128)S(1)} %fusion.10), custom_call_target="InvertDiagBlocksLowerTriangular" | custom-call | tf_op jit(solution)/shard_map/jit(_solve_triangular)/triangular_solve | solution.py:12
  350.5 8.3 %fusion = f32[64,11,8,128]{3,0,2,1:T(8,128)} fusion(f32[11,125,8,128]{3,2,1,0:T(8,128)} %copy-done.1, f32[64,500]{1,0:T(8,128)S(1)} %fusion.2, s32[]{:T(128)S(6)} %select_n.6), kind=kOutput, calls=%fused_computation | convolution fusion | flops 1081344000 | bytes 8548356 | tf_op jit(solution)/shard_map/dot_general | solution.py:29
  358.8 34.4 %reduce-scatter.2.cloned.1.call-done = f32[16,11,8,128]{3,0,2,1:T(8,128)} async-done(((f32[64,11,8,128]{3,0,2,1:T(8,128)}), f32[16,11,8,128]{3,0,2,1:T(8,128)}) %reduce-scatter.2.cloned.1.call-update) | async-done | bytes 720912 | tf_op jit(solution)/shard_map/reduce_scatter | solution.py:28
  393.2 2.2 copy.30
  (27 shorter events, 4.2 us)
Async XLA Ops:
  7.2 301.7 %copy-start = (f32[500,64]{0,1:T(8,128)S(1)}, f32[500,64]{0,1:T(8,128)}, u32[]{:S(2)}) copy-start(f32[500,64]{0,1:T(8,128)} %param.8) | copy-start | bytes 384004
  7.2 289.6 %all-gather.4.cloned.1.call-start = ((), (), s32[]{:S(2)}) async-start(), calls=%async_computation.3 | async-start | bytes 34062336 | tf_op jit(solution)/shard_map/all_gather | solution.py:21
  10.3 2.5 copy-start.1
  104.5 288.7 %reduce-scatter.2.cloned.1.call-start = ((), (), s32[]{:S(2)}) async-start(), calls=%async_computation.2 | async-start | bytes 3604480 | tf_op jit(solution)/shard_map/reduce_scatter | solution.py:28
  350.5 8.3 %copy-start.2 = (f32[64,500]{1,0:T(8,128)}, f32[64,500]{1,0:T(8,128)S(1)}, u32[]{:S(2)}) copy-start(f32[64,500]{1,0:T(8,128)S(1)} %fusion.2) | copy-start | bytes 384004
Sparse Core Ops, SparseCore 0:
  104.6 192.0 all-gather.3
  358.9 34.2 reduce-scatter.1
